TPU v7x, 256 devices: a 8x8x2 block of a 8x8x16 slice. The times are simulated.
256 devices in a mesh: groups: 2 (over z), seq: 128 (over x, y, core).
Axes of the slice: x: 8, y: 8, z: 2, core: 2. Of those that a mesh axis runs over, the one named last changes fastest.
The devices are a block of a 8x8x16 slice.
Arguments:
- latents: bfloat16 [2048, 64, 640], P(('groups', 'seq')), parts along dimension 0, may hold values from -6 to 6
- norm_gain: float32 [640], replicated, may hold values from 0.25 to 1.75
- norm_bias: float32 [640], replicated, may hold values from -3 to 3
- conv_weight: bfloat16 [5760, 640], P('seq'), may hold values from -0.078125 to 0.078125
- time_weight: bfloat16 [320, 640], replicated, may hold values from -0.3125 to 0.3125
- first_gain: float32 [640], replicated, may hold values from 0.25 to 1.75
- tconv_weight: bfloat16 [1920, 640], P('seq'), may hold values from -0.125 to 0.125
- second_gain: float32 [640], replicated, may hold values from 0.25 to 1.75
- qkv_weight: bfloat16 [640, 1920], P('seq'), may hold values from -0.25 to 0.25
- out_weight: bfloat16 [640, 640], P('seq'), may hold values from -0.25 to 0.25
- timesteps: int32 [8], P('groups'), parts along dimension 0, may hold values from 0 to 999
Outputs:
- mixed: bfloat16 [2048, 64, 640], P(('groups', 'seq')), parts along dimension 0
There are 2 independent parts, one for each index of `groups`. A program takes and returns all parts, laid end to end along the dimension named above; an argument that names none is the same for every part. Nothing has to cross between parts.
All inputs are finite; a program needn't handle non-finite values.
Results may differ from a plain program's by a relative error of at most 0.008.
Values may be sent and summed in bfloat16 or wider, within the bound.
No kernel may reach another device: no remote copies, remote signals or barrier semaphores. Data moves between devices by JAX's collectives and lax.ppermute only.
A program may use at most 128 MiB of HBM per device.

v0:
```python
import functools

import jax
import jax.numpy as jnp
from jax import lax
from jax.sharding import Mesh
from jax.sharding import PartitionSpec as P

HEAD = 64
GROUPS = 32
TFEAT = 320
FRAMES = 16
SEQ = ("seq_0", "seq_1", "seq_2")
GROUPS_SEQ = ("groups", "seq_0", "seq_1", "seq_2")


def in_order(parts, dim):
    dims = list(parts.shape[1:])
    dims[dim] *= parts.shape[0]
    return jnp.moveaxis(parts, 0, dim).reshape(dims)


def one_gather(arrays, axis, dims):
    ravelled = jnp.concatenate([a.reshape(-1) for a in arrays])
    lines, at, gathered = (lax.all_gather(ravelled, axis), 0, [])
    for a, dim in zip(arrays, dims):
        parts = lines[:, at : at + a.size].reshape(-1, *a.shape)
        gathered.append(in_order(parts, dim))
        at += a.size
    return tuple(gathered)


def one_axis_at_a_time(shard, axes):
    return functools.reduce(lax.psum, axes, shard)


def from_behind(block, axis, distance):
    devices = range(lax.axis_size(axis))
    route = [(i - distance, i) for i in devices if i - distance in devices]
    return lax.ppermute(block, axis, route)


def time_embed(timesteps, time_weight):
    half = TFEAT // 2
    freqs = jnp.exp(-jnp.log(10000.0) * jnp.arange(half, dtype=jnp.float32) / half)
    angles = timesteps.astype(jnp.float32)[:, None] * freqs[None, :]
    feats = jnp.concatenate([jnp.cos(angles), jnp.sin(angles)], axis=-1)
    return jnp.dot(feats, time_weight.astype(jnp.float32))


def layer_norm(values):
    mean = jnp.mean(values, axis=-1, keepdims=True)
    centered = values - mean
    var = jnp.mean(centered * centered, axis=-1, keepdims=True)
    return centered * lax.rsqrt(var + 1e-05)


def temporal_block(spatial, first_gain, tconv_weight, second_gain, qkv_weight, out_weight):
    clips, frames, places, chans = spatial.shape
    heads = chans // HEAD
    values = spatial.astype(jnp.float32)
    first = (layer_norm(values) * first_gain).astype(jnp.bfloat16)
    zero = jnp.zeros_like(first[:, :1])
    before = jnp.concatenate([zero, first[:, :-1]], axis=1)
    after = jnp.concatenate([first[:, 1:], zero], axis=1)
    stacked = jnp.concatenate([before, first, after], axis=-1).reshape(-1, 3 * chans)
    mid = values + jnp.dot(stacked, tconv_weight, preferred_element_type=jnp.float32).reshape(
        values.shape
    )
    second = (layer_norm(mid) * second_gain).astype(jnp.bfloat16)
    qkv = jnp.dot(second.reshape(-1, chans), qkv_weight, preferred_element_type=jnp.float32).astype(
        jnp.bfloat16
    )
    qkv = qkv.reshape(clips, frames, places, 3, heads, HEAD)
    query, key, value = (qkv[:, :, :, 0], qkv[:, :, :, 1], qkv[:, :, :, 2])
    scores = jnp.einsum(
        "cfphd,cgphd->cphfg", query, key, preferred_element_type=jnp.float32
    ) * HEAD ** (-0.5)
    weights = jax.nn.softmax(scores, axis=-1).astype(jnp.bfloat16)
    attended = jnp.einsum(
        "cphfg,cgphd->cfphd", weights, value, preferred_element_type=jnp.float32
    ).astype(jnp.bfloat16)
    projected = jnp.dot(attended.reshape(-1, chans), out_weight, preferred_element_type=jnp.float32)
    return (mid + projected.reshape(mid.shape)).astype(jnp.bfloat16)


def shards(
    latents,
    norm_gain,
    norm_bias,
    conv_weight,
    time_weight,
    first_gain,
    tconv_weight,
    second_gain,
    qkv_weight,
    out_weight,
    timesteps,
):
    devices = lax.axis_size(SEQ)
    device = lax.axis_index(SEQ)
    clips = timesteps.shape[0]
    images = clips * FRAMES
    sharing = devices // images
    rows, width, chans = latents.shape
    height = sharing * rows
    image = device % images
    clip = image // FRAMES
    tconv_full, qkv_full, out_full = one_gather(
        (tconv_weight, qkv_weight, out_weight), SEQ, (0, 0, 0)
    )
    temb_all = time_embed(timesteps, time_weight)
    pick = (jnp.arange(clips) == clip).astype(jnp.float32)
    temb = jnp.sum(pick[:, None] * temb_all, axis=0)
    values = latents.astype(jnp.float32).reshape(rows * width, GROUPS, chans // GROUPS)
    partial_sums = jnp.stack([jnp.sum(values, axis=(0, 2)), jnp.sum(values * values, axis=(0, 2))])
    owner = (jnp.arange(images) == image).astype(jnp.float32)
    table = one_axis_at_a_time(owner[:, None, None] * partial_sums[None], SEQ)
    mine = jnp.sum(owner[:, None, None] * table, axis=0)
    entries = height * width * (chans // GROUPS)
    mean = mine[0] / entries
    var = mine[1] / entries - mean * mean
    normed = (values - mean[None, :, None]) * lax.rsqrt(var + 1e-05)[None, :, None]
    normed = normed.reshape(rows, width, chans) * norm_gain + norm_bias
    normed = jax.nn.silu(normed).astype(jnp.bfloat16)
    upper_rim = from_behind(normed[rows - 1 :], SEQ, images)
    lower_rim = from_behind(normed[:1], SEQ, -images)
    padded = jnp.concatenate([upper_rim, normed, lower_rim], axis=0)
    padded = jnp.pad(padded, ((0, 0), (1, 1), (0, 0)))
    taps = [padded[dy : dy + rows, dx : dx + width] for dy in range(3) for dx in range(3)]
    columns = jnp.concatenate(taps, axis=-1).reshape(rows * width, 9 * chans)
    base = latents.reshape(rows * width, chans).astype(jnp.float32) + temb[None, :]
    conv = jnp.dot(
        columns,
        lax.all_gather(conv_weight, SEQ, axis=0, tiled=True),
        preferred_element_type=jnp.float32,
    )
    spatial = (base + conv).astype(jnp.bfloat16)
    moved = lax.all_to_all(spatial, SEQ, split_axis=0, concat_axis=0, tiled=True)
    block = rows * width // devices
    places = sharing * block
    ordered = jnp.transpose(moved.reshape(sharing, clips, FRAMES, block, chans), (1, 2, 0, 3, 4))
    grouped = ordered.reshape(clips, FRAMES, places, chans)
    result = temporal_block(grouped, first_gain, tconv_full, second_gain, qkv_full, out_full)
    unordered = jnp.transpose(result.reshape(clips, FRAMES, sharing, block, chans), (2, 0, 1, 3, 4))
    returned = lax.all_to_all(
        unordered.reshape(rows * width, chans), SEQ, split_axis=0, concat_axis=0, tiled=True
    )
    return returned.reshape(rows, width, chans)


def solution(mesh):
    torus = Mesh(
        mesh.devices.reshape(mesh.shape["groups"], 8, 8, 2), ("groups", "seq_0", "seq_1", "seq_2")
    )
    return jax.shard_map(
        shards,
        mesh=torus,
        in_specs=(
            P(GROUPS_SEQ, None, None),
            P(),
            P(),
            P(SEQ, None),
            P(),
            P(),
            P(SEQ, None),
            P(),
            P(SEQ, None),
            P(SEQ, None),
            P("groups"),
        ),
        out_specs=P(GROUPS_SEQ, None, None),
        check_vma=False,
    )
```

profile of v0, /device:TPU:513, one launch (start us, length us, event | category | flops | bytes accessed | tf_op | source)
XLA Modules:
  0.0 346.2 jit_solution(1874407834715782001)
XLA Ops:
  6.6 0.8 reshape.144
  7.4 0.8 reshape.145
  8.2 0.7 reshape.146
  9.0 0.7 reshape.158
  9.8 0.7 all-gather.6.cloned.1.call-update
  10.5 1.3 convert_reduce_fusion
  12.4 24.3 %psum.21 = f32[64,2,32]{0,2,1:T(8,128)S(1)} all-reduce(f32[64,2,32]{0,2,1:T(8,128)S(1)} %broadcast_multiply_fusion.1), channel_id=1, replica_groups=mesh['groups'=2,'seq_0'=8,'seq_1'=8,'seq_2'=2] {'seq_0'}, use_global_device_ids=true, to_apply=%region_5.6 | all-reduce | flops 4096 | bytes 32768 | tf_op jit(solution)/shard_map/psum | solution.py:34
  36.7 33.6 %psum.22 = f32[64,2,32]{0,2,1:T(8,128)S(1)} all-reduce(f32[64,2,32]{0,2,1:T(8,128)S(1)} %psum.21), channel_id=1, replica_groups=mesh['groups'=2,'seq_0'=8,'seq_1'=8,'seq_2'=2] {'seq_1'}, use_global_device_ids=true, to_apply=%region_6.7 | all-reduce | flops 4096 | bytes 32768 | tf_op jit(solution)/shard_map/psum | solution.py:34
  70.3 20.2 %psum.23 = f32[64,2,32]{0,2,1:T(8,128)S(1)} all-reduce(f32[64,2,32]{0,2,1:T(8,128)S(1)} %psum.22), channel_id=1, replica_groups=mesh['groups'=2,'seq_0'=8,'seq_1'=8,'seq_2'=2] {'seq_2'}, use_global_device_ids=true, to_apply=%region_7.8 | all-reduce | flops 4096 | bytes 32768 | tf_op jit(solution)/shard_map/psum | solution.py:34
  91.0 1.2 multiply_convert_fusion.2
  92.2 2.6 collective-permute-start
  94.8 1.3 collective-permute-start.1
  96.2 0.1 multiply_cosine_fusion
  96.3 0.2 fusion.29
  96.6 1.9 collective-permute-done
  98.5 9.0 %collective-permute-done.1 = bf16[1,64,640]{2,1,0:T(8,128)(2,1)S(1)} collective-permute-done((bf16[1,64,640]{2,1,0:T(8,128)(2,1)S(1)}, bf16[1,64,640]{2,1,0:T(8,128)(2,1)S(1)}, u32[]{:S(2)}, u32[]{:S(2)}) %collective-permute-start.1) | collective-permute-done | bytes 81952 | tf_op jit(solution)/shard_map/ppermute | solution.py:40
  107.6 0.3 fusion.35
  107.8 1.0 slice_dynamic-update-slice_fusion.5
  108.8 0.9 fusion.39
  109.7 1.0 slice_dynamic-update-slice_fusion.4
  110.8 1.0 slice_dynamic-update-slice_fusion.3
  111.7 1.3 constant_dynamic-update-slice_fusion
  113.1 1.1 slice_dynamic-update-slice_fusion.2
  114.1 1.0 slice_dynamic-update-slice_fusion.1
  115.1 1.0 fusion.38
  116.1 1.1 slice_dynamic-update-slice_fusion
  117.1 2.4 all-gather.8.cloned.1.call-done
  119.6 4.9 %copy.139 = bf16[128,1,22400]{2,0,1:T(8,128)(2,1)S(1)} copy(bf16[128,1,22400]{2,1,0:T(2,128)(2,1)} %all-gather.8.cloned.1.call-done) | data formatting | bytes 11468800
  124.4 2.4 copy-done.2
  126.9 76.5 %all-gather.6.cloned.1.call-done = bf16[128,45,640]{2,1,0:T(8,128)(2,1)} async-done(((bf16[1,45,640]{2,1,0:T(8,128)(2,1)}), bf16[128,45,640]{2,1,0:T(8,128)(2,1)}) %all-gather.6.cloned.1.call-update) | async-done | bytes 7372816 | tf_op jit(solution)/shard_map/all_gather | solution.py:135
  203.5 9.3 %reshape.157 = bf16[5760,640]{1,0:T(8,128)(2,1)} reshape(bf16[128,45,640]{2,1,0:T(8,128)(2,1)} %all-gather.6.cloned.1.call-done) | data formatting | bytes 14745600
  212.8 9.6 %fusion.24 = bf16[512,640]{1,0:T(8,128)(2,1)S(1)} fusion(f32[512,640]{1,0:T(8,128)S(1)} %bitcast_add_fusion, bf16[512,5760]{1,0:T(8,128)(2,1)} %bitcast.5, bf16[5760,640]{1,0:T(8,128)(2,1)} %reshape.157), kind=kOutput, calls=%fused_computation.28 | convolution fusion | flops 3775528960 | bytes 15237120 | tf_op jit(solution)/shard_map/dot_general | solution.py:133
  222.4 1.0 all_to_all.12
  223.4 11.5 %all-to-all-start = ((bf16[128,4,640]{2,1,0:T(4,128)(2,1)}), bf16[128,4,640]{2,1,0:T(4,128)(2,1)}, u32[]{:S(2)}, u32[]{:S(2)}) async-start(bf16[128,4,640]{2,1,0:T(4,128)(2,1)} %all_to_all.12), calls=%async_computation | async-start | bytes 1310720 | tf_op jit(solution)/shard_map/all_to_all | solution.py:139
  234.9 4.2 %fusion.54 = (bf16[128,9600]{1,0:T(8,128)(2,1)S(1)}, bf16[128,9600]{1,0:T(8,128)(2,1)}) fusion(bf16[128,22400]{1,0:T(8,128)(2,1)} %bitcast.64), kind=kLoop, calls=%fused_computation.95 | loop fusion | bytes 9830400 | tf_op jit(solution)/shard_map/slice | solution.py:27
  239.1 6.1 %reshape.161 = bf16[1920,640,1,1]{1,0,2,3:T(8,128)(2,1)} reshape(bf16[128,9600]{1,0:T(8,128)(2,1)} %get-tuple-element.11) | data formatting | bytes 4915200 | tf_op jit(solution)/shard_map/reshape;reshape | solution.py:20
  245.1 3.5 %reshape_reshape.10 = bf16[640,1920]{1,0:T(8,128)(2,1)} reshape(bf16[128,9600]{1,0:T(8,128)(2,1)S(1)} %get-tuple-element.10) | data formatting | bytes 4915200 | tf_op jit(solution)/shard_map/reshape;reshape | solution.py:20
  248.6 0.6 reshape.162
  249.2 7.5 %all-to-all-done = bf16[128,4,640]{2,1,0:T(4,128)(2,1)} async-done(((bf16[128,4,640]{2,1,0:T(4,128)(2,1)}), bf16[128,4,640]{2,1,0:T(4,128)(2,1)}, u32[]{:S(2)}, u32[]{:S(2)}) %all-to-all-start) | async-done | bytes 655392 | tf_op jit(solution)/shard_map/all_to_all | solution.py:139
  256.7 1.2 fusion.56
  257.9 0.2 fusion.37
  258.1 0.3 multiply_reduce_fusion.2
  258.6 1.9 copy.98
  260.5 1.7 reshape.152
  262.3 0.2 multiply_convert_fusion.1
  262.7 0.6 copy-done.4
  263.3 1.1 copy-done.6
  264.4 3.2 fusion.58
  267.7 0.3 multiply_reduce_fusion.1
  268.0 0.2 multiply_convert_fusion
  268.3 1.1 copy-done.5
  269.4 3.0 convolution_convert_fusion
  272.4 7.5 %reshape.148 = bf16[4,16,8,3,10,64]{5,4,3,2,1,0:T(8,128)(2,1)} reshape(bf16[512,1920]{1,0:T(8,128)(2,1)} %convolution_convert_fusion) | data formatting | bytes 3932160 | tf_op jit(solution)/shard_map/reshape | solution.py:74
  279.9 5.6 %fusion.53 = (bf16[4,16,8,1,10,64]{5,4,3,2,1,0:T(8,128)(2,1)S(1)}, bf16[4,16,8,1,10,64]{5,4,3,2,1,0:T(8,128)(2,1)S(1)}, bf16[4,16,8,1,10,64]{5,4,3,2,1,0:T(8,128)(2,1)S(1)}) fusion(bf16[4,16,8,3,10,64]{5,4,3,2,1,0:T(8,128)(2,1)} %reshape.148), kind=kLoop, calls=%fused_computation.94 | loop fusion | bytes 3932160 | tf_op jit(solution)/shard_map/slice | solution.py:75
  285.5 1.6 fusion.26
  287.1 11.1 %fusion.59 = (f32[4,8,10,16]{3,2,1,0:T(8,128)S(1)}, f32[4,8,10,16,16]{3,4,2,1,0:T(8,128)S(1)}) fusion(f32[4,8,10,16,16]{3,4,2,1,0:T(8,128)S(1)} %fusion.26), kind=kOutput, calls=%fused_computation.100 | output fusion | flops 327695 | bytes 675840 | tf_op jit(solution)/shard_map/sub | solution.py:79
  298.3 1.0 fusion.18
  299.3 1.9 copy.110
  301.3 3.0 dot_general.29
  304.2 1.6 fusion.25
  305.8 1.6 reshape.149
  307.5 0.5 copy.112
  308.0 30.4 %all_to_all.18 = bf16[128,4,640]{2,1,0:T(4,128)(2,1)S(1)} all-to-all(bf16[128,4,640]{2,1,0:T(4,128)(2,1)S(1)} %copy.112), channel_id=1, replica_groups=mesh['groups'=2,'seq_0'=8,'seq_1'=8,'seq_2'=2] {'seq_0','seq_1','seq_2'}, dimensions={0} | all-to-all | bytes 1310720 | tf_op jit(solution)/shard_map/all_to_all | solution.py:146
  338.4 1.0 reshape.150
  (53 shorter events, 1.7 us)
Async XLA Ops:
  6.5 89.8 %copy-start = (bf16[320,640]{1,0:T(8,128)(2,1)S(1)}, bf16[320,640]{1,0:T(8,128)(2,1)}, u32[]{:S(2)}) copy-start(bf16[320,640]{1,0:T(8,128)(2,1)} %param.15) | copy-start | bytes 1228804
  6.6 84.5 %copy-start.3 = (bf16[8,64,640]{2,1,0:T(8,128)(2,1)S(1)}, bf16[8,64,640]{2,1,0:T(8,128)(2,1)}, u32[]{:S(2)}) copy-start(bf16[8,64,640]{2,1,0:T(8,128)(2,1)} %param.11) | copy-start | bytes 1966084
  6.6 89.6 %copy-start.11 = (s32[4]{0:T(128)S(1)}, s32[4]{0:T(128)}, u32[]{:S(2)}) copy-start(s32[4]{0:T(128)} %param.21) | copy-start | bytes 52
  6.6 113.0 %all-gather.8.cloned.1.call-start = ((), (), s32[]{:S(2)}) async-start(), calls=%async_computation.3 | async-start | bytes 11558400 | tf_op jit(solution)/shard_map/all_gather | solution.py:25
  9.7 193.8 %all-gather.6.cloned.1.call-start = ((), (), s32[]{:S(2)}) async-start(), calls=%async_computation.2 | async-start | bytes 7925760 | tf_op jit(solution)/shard_map/all_gather | solution.py:135
  92.2 6.3 %collective-permute-start = (bf16[1,64,640]{2,1,0:T(8,128)(2,1)S(1)}, bf16[1,64,640]{2,1,0:T(8,128)(2,1)S(1)}, u32[]{:S(2)}, u32[]{:S(2)}) collective-permute-start(bf16[1,64,640]{2,1,0:T(8,128)(2,1)S(1)} %get-tuple-element.16), channel_id=1, source_target_pairs={{0,64},{1,65},{2,66},{3,67},{4,68},{5,69},{6,70},{7,71},{8,72},{9,... | collective-permute-start | bytes 245768 | tf_op jit(solution)/shard_map/ppermute | solution.py:40
  94.8 12.8 %collective-permute-start.1 = (bf16[1,64,640]{2,1,0:T(8,128)(2,1)S(1)}, bf16[1,64,640]{2,1,0:T(8,128)(2,1)S(1)}, u32[]{:S(2)}, u32[]{:S(2)}) collective-permute-start(bf16[1,64,640]{2,1,0:T(8,128)(2,1)S(1)} %get-tuple-element.17), channel_id=1, source_target_pairs={{64,0},{65,1},{66,2},{67,3},{68,4},{69,5},{70,6},{71,7},{72,8},{73... | collective-permute-start | bytes 245768 | tf_op jit(solution)/shard_map/ppermute | solution.py:40
  108.8 2.9 copy-start.7
  108.8 2.9 copy-start.8
  124.4 2.4 copy-start.2
  223.4 33.3 %all-to-all-start = ((bf16[128,4,640]{2,1,0:T(4,128)(2,1)}), bf16[128,4,640]{2,1,0:T(4,128)(2,1)}, u32[]{:S(2)}, u32[]{:S(2)}) async-start(bf16[128,4,640]{2,1,0:T(4,128)(2,1)} %all_to_all.12), calls=%async_computation | async-start | bytes 1310720 | tf_op jit(solution)/shard_map/all_to_all | solution.py:139
  260.5 1.8 copy-start.9
  262.3 1.1 copy-start.4
  262.3 2.1 copy-start.6
  264.4 3.6 %copy-start.10 = (f32[640]{0:T(1024)S(1)}, f32[640]{0:T(1024)}, u32[]{:S(2)}) copy-start(f32[640]{0:T(1024)} %param.18) | copy-start | bytes 7684
  267.7 1.7 copy-start.5
  307.5 31.9 %copy-start.1 = (bf16[320,640]{1,0:T(8,128)(2,1)S(1)}, bf16[320,640]{1,0:T(8,128)(2,1)}, u32[]{:S(2)}) copy-start(bf16[320,640]{1,0:T(8,128)(2,1)} %param.15) | copy-start | bytes 1228804
Sparse Core Ops, SparseCore 0:
  10.0 109.5 all-gather.7
  122.2 81.2 all-gather.5
where the time goes:
time: 348 us; the launch traced here: 346 us
  blocking collectives  109 us (31%)
  waiting for transfers between devices  98.1 us (28%)
  local copies, waits for them, and re-layouts  69.6 us (20%)
  matrix products  20.4 us (6%)
  other arithmetic  20.3 us (6%)
  starting transfers between devices  15.4 us (4%)
  between operations  13.9 us (4%)
    psum x3, blocking collectives, one_axis_at_a_time(): return functools.reduce(lax.psum, axes, shard)  78.2 us
    all_gather x1, waiting for transfers between devices, shards(): lax.all_gather(conv_weight, SEQ, axis=0, tiled=True)  76.5 us
    all_to_all x1, blocking collectives, shards(): lax.all_to_all(unordered.reshape(rows * width, chans), SEQ, split_axis=0,...  30.4 us
    unnamed x32, local copies, waits for them, and re-layouts  25.2 us
    all_to_all x1, starting transfers between devices, shards(): lax.all_to_all(spatial, SEQ, split_axis=0, concat_axis=0, tiled=True)  11.5 us
    sub x1, other arithmetic, temporal_block(): weights = jax.nn.softmax(scores, axis=-1).astype(jnp.bfloat16)  11.1 us
    ppermute x2, waiting for transfers between devices, from_behind(): return lax.ppermute(block, axis, route)  10.9 us
    another operation x3, local copies, waits for them, and re-layouts, in_order(): return jnp.moveaxis(parts, 0, dim).reshape(dims)  10.1 us
  transfers between devices with their start and end apart: 5, of which 5 were waited for; matrix products, arithmetic and copies ran while one was open for 9% of the time, Pallas kernels for 0%

commit v1 on v0

v1 whole, which is shorter than its diff:
```python
import jax
import jax.numpy as jnp
from jax import lax
from jax.experimental import pallas as pl
from jax.experimental.pallas import tpu as pltpu
from jax.sharding import Mesh
from jax.sharding import PartitionSpec as P

HEAD = 64
GROUPS = 32
TFEAT = 320
FRAMES = 16
SEQ = ("seq_0", "seq_1", "seq_2")
GROUPS_SEQ = ("groups", "seq_0", "seq_1", "seq_2")
SIDE = 8
CONV_BLOCK = 48
TCONV_BLOCK = 16
VMEM_LIMIT = 56 * 2**20
OFFSETS = (0, -1, -2, -3, -4, 1, 2, 3)
FIRST_SWAP = (0, 1, 2, 5, 6)
SECOND_SWAP = (3, 4, 7)


def route(target):
    pairs = []
    for x in range(SIDE):
        for y in range(SIDE):
            for core in range(2):
                there = target(x, y, core)
                if there is not None:
                    tx, ty, tcore = there
                    to = (tx % SIDE * SIDE + ty % SIDE) * 2 + tcore
                    pairs.append(((x * SIDE + y) * 2 + core, to))
    return pairs


def send(block, target):
    return lax.ppermute(block, SEQ, route(target))


def inner(step):
    return lambda x, y, core: (x + step, y, core) if core == 0 else (x, y + step, core)


def outer(step):
    return lambda x, y, core: (x, y + step, core) if core == 0 else (x + step, y, core)


def swap(x, y, core):
    return x, y, 1 - core


def ring(block, towards):
    ahead, behind = [block], [block]
    for step in range(SIDE // 2):
        ahead.append(send(ahead[-1], towards(1)))
        if step < SIDE // 2 - 1:
            behind.append(send(behind[-1], towards(-1)))
    return ahead + behind[1:]


def time_embed(timestep, time_weight):
    half = TFEAT // 2
    freqs = jnp.exp(-jnp.log(10000.0) * jnp.arange(half, dtype=jnp.float32) / half)
    angles = timestep.astype(jnp.float32)[None, None] * freqs[None, :]
    feats = jnp.concatenate([jnp.cos(angles), jnp.sin(angles)], axis=-1)
    return jnp.dot(feats, time_weight.astype(jnp.float32), precision=lax.Precision.HIGHEST)


def wrap(value):
    return lax.rem(value + 2 * SIDE, SIDE)


def offset_of(slot):
    return jnp.where(slot <= SIDE // 2, -slot, slot - SIDE // 2)


def piece_refs(mine, first, second):
    other = {}
    for i, at in enumerate(FIRST_SWAP):
        other[at] = first.at[i]
    for i, at in enumerate(SECOND_SWAP):
        other[at] = second.at[i]
    return [(0, i, mine[i]) for i in range(SIDE)] + [(1, i, other[i]) for i in range(SIDE)]


def fetch_blocks(where, pieces, weight, size, sem):
    x, y, core = where[0], where[1], where[2]
    for swapped, slot, ref in pieces:
        holder = core if swapped == 0 else 1 - core
        across = OFFSETS[slot]

        def one(b, carry, ref=ref, holder=holder, across=across):
            along = offset_of(b)
            px = wrap(x + jnp.where(holder == 0, along, across))
            py = wrap(y + jnp.where(holder == 0, across, along))
            inside = 2 * py + holder

            @pl.when(inside < 2 * SIDE - 1)
            def _():
                at = pl.multiple_of((px * (2 * SIDE - 1) + inside) * size, size)
                source = ref.at[pl.ds(pl.multiple_of(b * size, size), size)]
                pltpu.make_async_copy(source, weight.at[pl.ds(at, size)], sem).start()

            return carry

        lax.fori_loop(0, SIDE, one, 0)


def conv_kernel(where, latents, halo, vectors, *refs):
    mine, (first, second, out, weight, shifted, total, sem) = refs[:SIDE], refs[SIDE:]
    fetch_blocks(where, piece_refs(mine, first, second), weight, CONV_BLOCK, sem)
    rows, width, chans = latents.shape
    mean, scale, bias = vectors[0:1, :], vectors[1:2, :], vectors[2:3, :]
    column = lax.broadcasted_iota(jnp.int32, (width, 1), 0)
    lower = where[3]

    def fill(at, raw):
        values = (raw.astype(jnp.float32) - mean) * scale + bias
        values = values / (1.0 + jnp.exp(-values))
        left = jnp.where(column == 0, 0.0, pltpu.roll(values, 1, 0))
        right = jnp.where(column == width - 1, 0.0, pltpu.roll(values, width - 1, 0))
        shifted[0, at] = left.astype(jnp.bfloat16)
        shifted[1, at] = values.astype(jnp.bfloat16)
        shifted[2, at] = right.astype(jnp.bfloat16)

    def one_row(r, carry):
        fill(r + 1, latents[r])
        return carry

    lax.fori_loop(0, rows, one_row, 0)
    fill(jnp.where(lower == 1, 0, rows + 1), halo[0])
    empty = jnp.where(lower == 1, rows + 1, 0)
    for dx in range(3):
        shifted[dx, empty] = jnp.zeros((width, chans), jnp.bfloat16)
    pltpu.make_async_copy(weight, weight, sem).wait()
    for tap in range(9):
        dy, dx = divmod(tap, 3)
        taken = shifted[dx, dy : dy + rows].reshape(rows * width, chans)
        part = jnp.dot(
            taken,
            weight[tap * chans : (tap + 1) * chans, :],
            preferred_element_type=jnp.float32,
        )
        if tap == 0:
            total[...] = part
        elif tap < 8:
            total[...] += part
        else:
            base = latents[...].astype(jnp.float32).reshape(rows * width, chans)
            out[...] = (base + (total[...] + part) + vectors[3:4, :]).astype(jnp.bfloat16)


def layer_norm(values):
    mean = jnp.mean(values, axis=-1, keepdims=True)
    centered = values - mean
    var = jnp.mean(centered * centered, axis=-1, keepdims=True)
    return centered * lax.rsqrt(var + 1e-05)


def temporal_kernel(where, moved, gains, *refs):
    mine = refs[:SIDE]
    first_swap, second_swap, out, tconv, dense, mid, qkv, attended, sem, dense_sem = refs[SIDE:]
    x, y, core = where[0], where[1], where[2]
    frames, places, chans = moved.shape
    pieces = piece_refs(mine, first_swap, second_swap)
    fetch_blocks(where, pieces, tconv, TCONV_BLOCK, sem)
    share = chans // SIDE
    for swapped, slot, ref in pieces:
        holder = core if swapped == 0 else 1 - core
        at = wrap(jnp.where(holder == 0, y, x) + OFFSETS[slot])
        for m in range(2):
            source = ref.at[pl.ds(SIDE * TCONV_BLOCK + m * share, share)]
            target = dense.at[2 * holder + m, pl.ds(pl.multiple_of(at * share, 16), share)]
            pltpu.make_async_copy(source, target, dense_sem).start()
    rows = frames * places
    values = moved[...].astype(jnp.float32).reshape(rows, chans)
    first = (layer_norm(values) * gains[0:1, :]).astype(jnp.bfloat16)
    zero = jnp.zeros((places, chans), jnp.bfloat16)
    before = jnp.concatenate([zero, first[:-places]], axis=0)
    after = jnp.concatenate([first[places:], zero], axis=0)
    pltpu.make_async_copy(tconv, tconv, sem).wait()
    mid[...] = values + jnp.dot(
        before, tconv[:chans, :], preferred_element_type=jnp.float32
    )
    mid[...] += jnp.dot(first, tconv[chans : 2 * chans, :], preferred_element_type=jnp.float32)
    mid[...] += jnp.dot(after, tconv[2 * chans :, :], preferred_element_type=jnp.float32)
    second = (layer_norm(mid[...]) * gains[1:2, :]).astype(jnp.bfloat16)
    pltpu.make_async_copy(dense, dense, dense_sem).wait()
    for m in range(3):
        part = jnp.dot(second, dense[m], preferred_element_type=jnp.float32)
        qkv[m] = part.astype(jnp.bfloat16).reshape(frames, places, chans)
    some = 16
    many = frames * some
    row_place = lax.broadcasted_iota(jnp.int32, (many, many), 0) % some
    col_place = lax.broadcasted_iota(jnp.int32, (many, many), 1) % some
    same = row_place == col_place
    lane = lax.broadcasted_iota(jnp.int32, (1, 2 * HEAD), 1)
    for group in range(places // some):
        spot = slice(group * some, (group + 1) * some)
        for pair in range(chans // (2 * HEAD)):
            lanes = slice(pair * 2 * HEAD, (pair + 1) * 2 * HEAD)
            query = qkv[0, :, spot, lanes].reshape(many, 2 * HEAD)
            key = qkv[1, :, spot, lanes].reshape(many, 2 * HEAD)
            value = qkv[2, :, spot, lanes].reshape(many, 2 * HEAD)
            both = []
            for side in range(2):
                own = (lane < HEAD) if side == 0 else (lane >= HEAD)
                only = jnp.where(own, query, jnp.zeros_like(query))
                scores = lax.dot_general(
                    only, key, (((1,), (1,)), ((), ())), preferred_element_type=jnp.float32
                )
                scores = jnp.where(same, scores * HEAD ** (-0.5), -1e30)
                top = jnp.max(scores, axis=-1, keepdims=True)
                raised = jnp.exp(scores - top)
                weights = raised / jnp.sum(raised, axis=-1, keepdims=True)
                both.append(
                    jnp.dot(weights.astype(jnp.bfloat16), value, preferred_element_type=jnp.float32)
                )
            mixed = jnp.where(lane < HEAD, both[0], both[1]).astype(jnp.bfloat16)
            attended[:, spot, lanes] = mixed.reshape(frames, some, 2 * HEAD)
    projected = jnp.dot(
        attended[...].reshape(rows, chans), dense[3], preferred_element_type=jnp.float32
    )
    out[...] = (mid[...] + projected).astype(jnp.bfloat16).reshape(frames, places, chans)


def specs(count):
    return [pl.BlockSpec(memory_space=pl.ANY)] * count


def shards(
    latents,
    norm_gain,
    norm_bias,
    conv_weight,
    time_weight,
    first_gain,
    tconv_weight,
    second_gain,
    qkv_weight,
    out_weight,
    timesteps,
):
    devices = lax.axis_size(SEQ)
    device = lax.axis_index(SEQ)
    x, y, core = (lax.axis_index(name) for name in SEQ)
    clips = timesteps.shape[0]
    images = clips * FRAMES
    sharing = devices // images
    rows, width, chans = latents.shape
    height = sharing * rows
    image = device % images
    clip = image // FRAMES
    lower = device // images
    bf16, f32 = jnp.bfloat16, jnp.float32

    conv_rows, tconv_rows = conv_weight.shape[0], tconv_weight.shape[0]
    both = jnp.concatenate([conv_weight, tconv_weight], axis=0)

    def to_previous(px, py, pcore):
        spot = 2 * py + pcore - 1
        return None if spot < 0 else (px, spot // 2, spot % 2)

    following = send(both, to_previous)
    inside = 2 * y + core
    conv_two = jnp.concatenate([both[:conv_rows], following[:conv_rows]], axis=0)
    tconv_two = jnp.concatenate([both[conv_rows:], following[conv_rows:]], axis=0)
    conv_at = jnp.minimum((CONV_BLOCK - conv_rows) * inside, 2 * conv_rows - CONV_BLOCK)
    tconv_at = jnp.minimum((TCONV_BLOCK - tconv_rows) * inside, 2 * tconv_rows - TCONV_BLOCK)
    conv_block = lax.dynamic_slice_in_dim(conv_two, conv_at, CONV_BLOCK, 0)
    tconv_block = lax.dynamic_slice_in_dim(tconv_two, tconv_at, TCONV_BLOCK, 0)

    few = qkv_weight.shape[0]
    query_key = jnp.concatenate([qkv_weight[:, :chans], qkv_weight[:, chans : 2 * chans]], axis=0)
    value_out = jnp.concatenate([qkv_weight[:, 2 * chans :], out_weight], axis=0)
    same_core = send(query_key, lambda px, py, pcore: (py, px, 0) if pcore == 0 else None)
    crossed = send(
        jnp.where(core == 0, value_out, query_key),
        lambda px, py, pcore: (px, py, 1) if pcore == 0 else (py, px, 0),
    )
    from_even = jnp.where(core == 0, same_core, crossed).reshape(2, few, chans)
    from_odd = jnp.where(core == 0, crossed, value_out).reshape(2, few, chans)
    dense_block = jnp.concatenate([from_even, from_odd], axis=1).reshape(4 * few, chans)

    pairs = [(i, (i + images) % devices) for i in range(devices)]
    edge = lax.dynamic_slice_in_dim(latents, jnp.where(lower == 1, 0, rows - 1), 1, 0)
    halo = lax.ppermute(edge, SEQ, pairs)
    values = latents.astype(f32).reshape(rows * width, chans)
    sums = jnp.stack([jnp.sum(values, axis=0), jnp.sum(values * values, axis=0)])
    sums = jnp.sum(sums.reshape(2, GROUPS, chans // GROUPS), axis=2)
    sums = sums + lax.ppermute(sums, SEQ, pairs)
    entries = height * width * (chans // GROUPS)
    mean = sums[0] / entries
    var = sums[1] / entries - mean * mean
    spread = lax.rsqrt(var + 1e-05)
    wide = lambda v: jnp.repeat(v, chans // GROUPS)
    temb = time_embed(lax.dynamic_index_in_dim(timesteps, clip, 0, False), time_weight)
    vectors = jnp.stack([wide(mean), wide(spread) * norm_gain, norm_bias, temb[0]])

    line = jnp.stack(ring(jnp.concatenate([conv_block, tconv_block, dense_block], axis=0), inner))
    order = jnp.array([OFFSETS.index((k + 4) % SIDE - 4) for k in range(SIDE)])
    along = jnp.where(core == 0, x, y)
    conv_line = line[:, :CONV_BLOCK].reshape(SIDE * CONV_BLOCK, chans)
    conv_pieces = ring(conv_line, outer)
    conv_first = send(jnp.stack([conv_pieces[i] for i in FIRST_SWAP]), swap)
    conv_second = send(jnp.stack([conv_pieces[i] for i in SECOND_SWAP]), swap)
    tconv_line = line[:, CONV_BLOCK : CONV_BLOCK + TCONV_BLOCK].reshape(SIDE * TCONV_BLOCK, chans)
    sorted_line = jnp.take(line[:, CONV_BLOCK + TCONV_BLOCK :], order[(jnp.arange(SIDE) - along) % SIDE], axis=0)
    sorted_line = sorted_line.reshape(SIDE, 2, 2 * few, chans)
    dense_line = jnp.transpose(sorted_line, (1, 0, 2, 3)).reshape(4 * few * SIDE, chans)
    rest_line = jnp.concatenate([tconv_line, dense_line], axis=0)
    rest_line, _ = lax.optimization_barrier((rest_line, conv_pieces[4]))
    rest_pieces = ring(rest_line, outer)
    rest_first = send(jnp.stack([rest_pieces[i] for i in FIRST_SWAP]), swap)
    rest_second = send(jnp.stack([rest_pieces[i] for i in SECOND_SWAP]), swap)

    where = jnp.stack([x, y, core, lower]).astype(jnp.int32)
    smem = pl.BlockSpec(memory_space=pltpu.SMEM)
    vmem = pl.BlockSpec(memory_space=pltpu.VMEM)
    params = pltpu.CompilerParams(vmem_limit_bytes=VMEM_LIMIT)
    spatial = pl.pallas_call(
        conv_kernel,
        out_shape=jax.ShapeDtypeStruct((rows * width, chans), bf16),
        in_specs=[smem, vmem, vmem, vmem] + specs(SIDE + 2),
        out_specs=vmem,
        scratch_shapes=[
            pltpu.VMEM((9 * chans, chans), bf16),
            pltpu.VMEM((3, rows + 2, width, chans), bf16),
            pltpu.VMEM((rows * width, chans), f32),
            pltpu.SemaphoreType.DMA,
        ],
        compiler_params=params,
        name="conv",
    )(where, latents, halo, vectors, *conv_pieces, conv_first, conv_second)
    moved = lax.all_to_all(spatial, SEQ[1:], split_axis=0, concat_axis=0, tiled=True)
    places = rows * width // FRAMES
    result = pl.pallas_call(
        temporal_kernel,
        out_shape=jax.ShapeDtypeStruct((FRAMES, places, chans), bf16),
        in_specs=[smem, vmem, vmem] + specs(SIDE + 2),
        out_specs=vmem,
        scratch_shapes=[
            pltpu.VMEM((3 * chans, chans), bf16),
            pltpu.VMEM((4, chans, chans), bf16),
            pltpu.VMEM((FRAMES * places, chans), f32),
            pltpu.VMEM((3, FRAMES, places, chans), bf16),
            pltpu.VMEM((FRAMES, places, chans), bf16),
            pltpu.SemaphoreType.DMA,
            pltpu.SemaphoreType.DMA,
        ],
        compiler_params=params,
        name="temporal",
    )(
        where,
        moved.reshape(FRAMES, places, chans),
        jnp.stack([first_gain, second_gain]),
        *rest_pieces,
        rest_first,
        rest_second,
    )
    returned = lax.all_to_all(
        result.reshape(rows * width, chans), SEQ[1:], split_axis=0, concat_axis=0, tiled=True
    )
    return returned.reshape(rows, width, chans)


def solution(mesh):
    torus = Mesh(
        mesh.devices.reshape(mesh.shape["groups"], SIDE, SIDE, 2),
        ("groups", "seq_0", "seq_1", "seq_2"),
    )
    return jax.shard_map(
        shards,
        mesh=torus,
        in_specs=(
            P(GROUPS_SEQ, None, None),
            P(),
            P(),
            P(SEQ, None),
            P(),
            P(),
            P(SEQ, None),
            P(),
            P(SEQ, None),
            P(SEQ, None),
            P("groups"),
        ),
        out_specs=P(GROUPS_SEQ, None, None),
        check_vma=False,
    )
```

time: 348 us -> 220 us (0.63)
  blocking collectives: 109 us -> 23.3 us
  starting transfers between devices: 15.4 us -> 87.4 us
  waiting for transfers between devices: 98.1 us -> 48.6 us
  local copies, waits for them, and re-layouts: 69.6 us -> 24.7 us
  Pallas kernels: 0 us -> 22.5 us
  matrix products: 20.4 us -> 0.31 us
  between operations: 13.9 us -> 1.14 us
  other arithmetic: 20.3 us -> 11.3 us
    all_gather x2 -> x0, waiting for transfers between devices: 79 us -> none  [the longest x1 76.5 us: shards(): lax.all_gather(conv_weight, SEQ, axis=0, tiled=True)]
    psum x3 -> x0, blocking collectives: 78.2 us -> none  [one_axis_at_a_time(): return functools.reduce(lax.psum, axes, shard)]
    ppermute x2 -> x30, starting transfers between devices: 3.87 us -> 74.5 us  [the longest x28 61.3 us: send(): return lax.ppermute(block, SEQ, route(target))]
    pallas_call x0 -> x2, Pallas kernels: none -> 22.5 us  [the longest x1 11.8 us: shards(): pl.pallas_call(temporal_kernel, out_shape=jax.ShapeDtypeStruct((FRAMES, p...]
    ppermute x2 -> x30, waiting for transfers between devices: 10.9 us -> 32.9 us  [the longest x28 30.4 us: send(): return lax.ppermute(block, SEQ, route(target))]
    dot_general x7 -> x1, matrix products: 20.4 us -> 0.31 us  [time_embed(): jnp.dot(feats, time_weight.astype(jnp.float32), precision=lax.Precision.H...]
    unnamed x32 -> x57, local copies, waits for them, and re-layouts: 25.2 us -> 9.88 us
    sub x1 -> x0, other arithmetic: 11.1 us -> none  [temporal_block(): weights = jax.nn.softmax(scores, axis=-1).astype(jnp.bfloat16)]
  transfers between devices with their start and end apart: 5 -> 31, of which waited for: 5 -> 14; matrix products, arithmetic and copies ran while one was open for 9% -> 14% of each run, Pallas kernels for 0% -> 5%
where the time goes in v1:
time: 220 us; the launch traced here: 219 us
  starting transfers between devices  87.4 us (40%)
  waiting for transfers between devices  48.6 us (22%)
  local copies, waits for them, and re-layouts  24.7 us (11%)
  blocking collectives  23.3 us (11%)
  Pallas kernels  22.5 us (10%)
  other arithmetic  11.3 us (5%)
    ppermute x28, starting transfers between devices, send(): return lax.ppermute(block, SEQ, route(target))  61.3 us
    ppermute x28, waiting for transfers between devices, send(): return lax.ppermute(block, SEQ, route(target))  30.4 us
    all_to_all x1, blocking collectives, shards(): lax.all_to_all(result.reshape(rows * width, chans), SEQ[1:], split_axis=0...  23.3 us
    all_to_all x1, waiting for transfers between devices, shards(): lax.all_to_all(spatial, SEQ[1:], split_axis=0, concat_axis=0, tiled=True)  15.7 us
    all_to_all x1, starting transfers between devices, shards(): lax.all_to_all(spatial, SEQ[1:], split_axis=0, concat_axis=0, tiled=True)  12.9 us
    pallas_call x1, Pallas kernels, shards(): pl.pallas_call(temporal_kernel, out_shape=jax.ShapeDtypeStruct((FRAMES, p...  11.8 us
    pallas_call x1, Pallas kernels, shards(): pl.pallas_call(conv_kernel, out_shape=jax.ShapeDtypeStruct((rows * width,...  10.7 us
    unnamed x57, local copies, waits for them, and re-layouts  9.88 us
  transfers between devices with their start and end apart: 31, of which 14 were waited for; matrix products, arithmetic and copies ran while one was open for 14% of the time, Pallas kernels for 5%

profile of v1, /device:TPU:513, one launch (start us, length us, event | category | flops | bytes accessed | tf_op | source)
XLA Modules:
  0.0 219.2 jit_solution(10923701538069133963)
XLA Ops:
  0.0 1.6 constant_dynamic-slice_fusion
  1.6 6.6 %collective-permute-start = (bf16[1,64,640]{2,1,0:T(8,128)(2,1)}, bf16[1,64,640]{2,1,0:T(8,128)(2,1)}, u32[]{:S(2)}, u32[]{:S(2)}) collective-permute-start(bf16[1,64,640]{2,1,0:T(8,128)(2,1)} %constant_dynamic-slice_fusion), channel_id=1, source_target_pairs={{0,64},{1,65},{2,66},{3,67},{4,68},{5,69},{6,70},{7,71},{8,72},{9,... | collective-permute-start | bytes 245768 | tf_op jit(solution)/shard_map/ppermute | solution.py:288
  8.1 0.7 fusion.14
  8.9 0.7 pad_maximum_fusion.6
  10.3 14.0 %collective-permute-start.4 = (bf16[10,640]{1,0:T(8,128)(2,1)S(1)}, bf16[10,640]{1,0:T(8,128)(2,1)S(1)}, u32[]{:S(2)}, u32[]{:S(2)}) collective-permute-start(bf16[10,640]{1,0:T(8,128)(2,1)S(1)} %get-tuple-element.15), channel_id=1, source_target_pairs={{0,1},{1,0},{2,3},{3,16},{4,5},{5,32},{6,7},{7,48},{8,9},{9,64},{1... | collective-permute-start | bytes 38408 | tf_op jit(solution)/shard_map/ppermute | solution.py:38
  24.2 0.9 pad_maximum_fusion.4
  25.1 2.0 collective-permute-start.2
  27.1 1.3 gather_fusion
  28.4 0.7 broadcast_select_fusion.1
  29.3 1.6 collective-permute-done.2
  30.9 0.8 fusion.2
  31.7 0.9 fusion.1
  32.8 2.6 %collective-permute-start.9 = (bf16[84,640]{1,0:T(8,128)(2,1)S(1)}, bf16[84,640]{1,0:T(8,128)(2,1)S(1)}, u32[]{:S(2)}, u32[]{:S(2)}) collective-permute-start(bf16[84,640]{1,0:T(8,128)(2,1)S(1)} %pad_maximum_fusion.3), channel_id=1, source_target_pairs={{0,112},{1,15},{2,114},{3,1},{4,116},{5,3},{6,118},{7,5},{8,120},{... | collective-permute-start | bytes 322568 | tf_op jit(solution)/shard_map/ppermute | solution.py:38
  35.4 2.4 %collective-permute-done.5 = bf16[84,640]{1,0:T(8,128)(2,1)S(1)} collective-permute-done((bf16[84,640]{1,0:T(8,128)(2,1)S(1)}, bf16[84,640]{1,0:T(8,128)(2,1)S(1)}, u32[]{:S(2)}, u32[]{:S(2)}) %collective-permute-start.5) | collective-permute-done | bytes 107552 | tf_op jit(solution)/shard_map/ppermute | solution.py:38
  37.9 3.6 %collective-permute-start.10 = (bf16[84,640]{1,0:T(8,128)(2,1)S(1)}, bf16[84,640]{1,0:T(8,128)(2,1)S(1)}, u32[]{:S(2)}, u32[]{:S(2)}) collective-permute-start(bf16[84,640]{1,0:T(8,128)(2,1)S(1)} %collective-permute-done.9), channel_id=1, source_target_pairs={{0,112},{1,15},{2,114},{3,1},{4,116},{5,3},{6,118},{7,5},{8,120},{... | collective-permute-start | bytes 322568 | tf_op jit(solution)/shard_map/ppermute | solution.py:38
  41.4 2.3 %collective-permute-done.6 = bf16[84,640]{1,0:T(8,128)(2,1)S(1)} collective-permute-done((bf16[84,640]{1,0:T(8,128)(2,1)S(1)}, bf16[84,640]{1,0:T(8,128)(2,1)S(1)}, u32[]{:S(2)}, u32[]{:S(2)}) %collective-permute-start.6) | collective-permute-done | bytes 107552 | tf_op jit(solution)/shard_map/ppermute | solution.py:38
  43.8 3.8 %collective-permute-start.7 = (bf16[84,640]{1,0:T(8,128)(2,1)S(1)}, bf16[84,640]{1,0:T(8,128)(2,1)S(1)}, u32[]{:S(2)}, u32[]{:S(2)}) collective-permute-start(bf16[84,640]{1,0:T(8,128)(2,1)S(1)} %collective-permute-done.6), channel_id=1, source_target_pairs={{0,16},{1,3},{2,18},{3,5},{4,20},{5,7},{6,22},{7,9},{8,24},{9,11},... | collective-permute-start | bytes 322568 | tf_op jit(solution)/shard_map/ppermute | solution.py:38
  47.6 1.0 collective-permute-done.10
  49.3 2.1 collective-permute-start.8
  51.5 3.1 %collective-permute-done.8 = bf16[84,640]{1,0:T(8,128)(2,1)S(1)} collective-permute-done((bf16[84,640]{1,0:T(8,128)(2,1)S(1)}, bf16[84,640]{1,0:T(8,128)(2,1)S(1)}, u32[]{:S(2)}, u32[]{:S(2)}) %collective-permute-start.8) | collective-permute-done | bytes 107552 | tf_op jit(solution)/shard_map/ppermute | solution.py:38
  54.8 1.1 collective-permute-start.12
  57.2 1.8 collective-permute-start.16
  59.2 5.8 %collective-permute-done.12.refs_1_ = bf16[384,640]{1,0:T(8,128)(2,1)S(1)} collective-permute-done((bf16[384,640]{1,0:T(8,128)(2,1)S(1)}, bf16[384,640]{1,0:T(8,128)(2,1)S(1)}, u32[]{:S(2)}, u32[]{:S(2)}) %collective-permute-start.12) | collective-permute-done | bytes 491552 | tf_op jit(solution)/shard_map/ppermute | solution.py:38
  65.6 0.7 slice.48
  66.3 2.2 %gather_fusion.1 = bf16[8,20,640]{2,1,0:T(8,128)(2,1)} fusion(bf16[8,20,640]{2,1,0:T(8,128)(2,1)} %slice.48, s32[1024]{0:T(1024)S(1)} %pad_clamp_fusion), kind=kCustom, calls=%fused_computation.1 | custom fusion | bytes 409632 | tf_op jit(solution)/shard_map/jit(_take)/gather | solution.py:309
  68.5 1.0 copy.15
  69.5 0.8 bitcast_dynamic-update-slice_fusion.4
  70.3 2.6 %collective-permute-start.17 = (bf16[384,640]{1,0:T(8,128)(2,1)S(1)}, bf16[384,640]{1,0:T(8,128)(2,1)}, u32[]{:S(2)}, u32[]{:S(2)}) collective-permute-start(bf16[384,640]{1,0:T(8,128)(2,1)S(1)} %collective-permute-done.16.refs_5_), channel_id=1, source_target_pairs={{0,14},{1,113},{2,0},{3,115},{4,2},{5,117},{6,4},{7,119},{8,6},{9,... | collective-permute-start | bytes 1474568 | tf_op jit(solution)/shard_map/ppermute | solution.py:38
  72.9 0.9 bitcast_dynamic-update-slice_fusion.3
  74.1 0.8 bitcast_dynamic-update-slice_fusion.2
  74.9 0.8 bitcast_dynamic-update-slice_fusion.1
  75.7 7.3 %collective-permute-done.14.refs_3_ = bf16[384,640]{1,0:T(8,128)(2,1)} collective-permute-done((bf16[384,640]{1,0:T(8,128)(2,1)S(1)}, bf16[384,640]{1,0:T(8,128)(2,1)}, u32[]{:S(2)}, u32[]{:S(2)}) %collective-permute-start.14) | collective-permute-done | bytes 491552 | tf_op jit(solution)/shard_map/ppermute | solution.py:38
  83.0 6.0 %collective-permute-start.15 = (bf16[384,640]{1,0:T(8,128)(2,1)}, bf16[384,640]{1,0:T(8,128)(2,1)S(1)}, u32[]{:S(2)}, u32[]{:S(2)}) collective-permute-start(bf16[384,640]{1,0:T(8,128)(2,1)} %collective-permute-done.14.refs_3_), channel_id=1, source_target_pairs={{0,2},{1,17},{2,4},{3,19},{4,6},{5,21},{6,8},{7,23},{8,10},{9,25},... | collective-permute-start | bytes 1474568 | tf_op jit(solution)/shard_map/ppermute | solution.py:38
  89.0 1.9 bitcast_dynamic-update-slice_fusion
  90.9 8.1 %collective-permute-start.19 = (bf16[5,384,640]{2,1,0:T(8,128)(2,1)}, bf16[5,384,640]{2,1,0:T(8,128)(2,1)S(1)}, u32[]{:S(2)}, u32[]{:S(2)}) collective-permute-start(bf16[5,384,640]{2,1,0:T(8,128)(2,1)} %bitcast_dynamic-update-slice_fusion), channel_id=1, source_target_pairs={{0,1},{1,0},{2,3},{3,2},{4,5},{5,4},{6,7},{7,6},{8,9},{9,8},{10,11... | collective-permute-start | bytes 7372808 | tf_op jit(solution)/shard_map/ppermute | solution.py:38
  99.1 0.9 slice.47
  100.1 0.8 copy.16
  100.8 1.7 reshape.150
  102.6 1.0 pad_maximum_fusion.2.refs_0_
  103.6 1.6 collective-permute-start.21
  105.5 1.3 collective-permute-start.25
  107.3 2.6 %pad_maximum_fusion = bf16[3,384,640]{2,1,0:T(8,128)(2,1)} fusion(bf16[1,384,640]{2,1,0:T(8,128)(2,1)} %bitcast.23, bf16[1,384,640]{2,1,0:T(8,128)(2,1)S(1)} %bitcast.81, bf16[1,384,640]{2,1,0:T(8,128)(2,1)} %bitcast.21), kind=kLoop, calls=%fused_computation.4 | loop fusion | flops 1474560 | bytes 2949120 | tf_op jit(solution)/shard_map/stack | solution.py:307
  109.9 2.5 %collective-permute-start.20 = (bf16[3,384,640]{2,1,0:T(8,128)(2,1)}, bf16[3,384,640]{2,1,0:T(8,128)(2,1)}, u32[]{:S(2)}, u32[]{:S(2)}) collective-permute-start(bf16[3,384,640]{2,1,0:T(8,128)(2,1)} %pad_maximum_fusion), channel_id=1, source_target_pairs={{0,1},{1,0},{2,3},{3,2},{4,5},{5,4},{6,7},{7,6},{8,9},{9,8},{10,11... | collective-permute-start | bytes 4423688 | tf_op jit(solution)/shard_map/ppermute | solution.py:38
  112.4 0.8 bitcast_dynamic-update-slice_fusion.9
  113.3 2.7 %collective-permute-start.26 = (bf16[288,640]{1,0:T(8,128)(2,1)S(1)}, bf16[288,640]{1,0:T(8,128)(2,1)S(1)}, u32[]{:S(2)}, u32[]{:S(2)}) collective-permute-start(bf16[288,640]{1,0:T(8,128)(2,1)S(1)} %collective-permute-done.25.refs_5_), channel_id=1, source_target_pairs={{0,14},{1,113},{2,0},{3,115},{4,2},{5,117},{6,4},{7,119},{8,6},{9,... | collective-permute-start | bytes 1105928 | tf_op jit(solution)/shard_map/ppermute | solution.py:38
  116.0 0.8 bitcast_dynamic-update-slice_fusion.8
  116.8 3.5 %collective-permute-done.22.refs_2_ = bf16[288,640]{1,0:T(8,128)(2,1)S(1)} collective-permute-done((bf16[288,640]{1,0:T(8,128)(2,1)S(1)}, bf16[288,640]{1,0:T(8,128)(2,1)S(1)}, u32[]{:S(2)}, u32[]{:S(2)}) %collective-permute-start.22) | collective-permute-done | bytes 368672 | tf_op jit(solution)/shard_map/ppermute | solution.py:38
  120.3 0.8 bitcast_dynamic-update-slice_fusion.7
  121.2 0.8 bitcast_dynamic-update-slice_fusion.6
  122.0 6.6 %collective-permute-start.1 = (f32[2,32]{1,0:T(2,128)S(1)}, f32[2,32]{1,0:T(2,128)S(1)}, u32[]{:S(2)}, u32[]{:S(2)}) collective-permute-start(f32[2,32]{1,0:T(2,128)S(1)} %maximum_reduce_fusion), channel_id=1, source_target_pairs={{0,64},{1,65},{2,66},{3,67},{4,68},{5,69},{6,70},{7,71},{8,72},{9,... | collective-permute-start | bytes 776 | tf_op jit(solution)/shard_map/ppermute | solution.py:292
  128.5 0.8 bitcast_dynamic-update-slice_fusion.5
  129.3 2.5 %collective-permute-done.1 = f32[2,32]{1,0:T(2,128)S(1)} collective-permute-done((f32[2,32]{1,0:T(2,128)S(1)}, f32[2,32]{1,0:T(2,128)S(1)}, u32[]{:S(2)}, u32[]{:S(2)}) %collective-permute-start.1) | collective-permute-done | bytes 288 | tf_op jit(solution)/shard_map/ppermute | solution.py:292
  131.8 2.3 %collective-permute-start.28 = (bf16[5,288,640]{2,1,0:T(8,128)(2,1)}, bf16[5,288,640]{2,1,0:T(8,128)(2,1)}, u32[]{:S(2)}, u32[]{:S(2)}) collective-permute-start(bf16[5,288,640]{2,1,0:T(8,128)(2,1)} %bitcast_dynamic-update-slice_fusion.5), channel_id=1, source_target_pairs={{0,1},{1,0},{2,3},{3,2},{4,5},{5,4},{6,7},{7,6},{8,9},{9,8},{10,11... | collective-permute-start | bytes 5529608 | tf_op jit(solution)/shard_map/ppermute | solution.py:38
  134.9 1.4 collective-permute-start.24
  137.4 1.4 copy-done.5
  138.8 10.7 %conv.1 = bf16[512,640]{1,0:T(8,128)(2,1)} custom-call(s32[4]{0:T(128)} %pad_add_fusion.where, bf16[8,64,640]{2,1,0:T(8,128)(2,1)} %latents.1, bf16[1,64,640]{2,1,0:T(8,128)(2,1)} %collective-permute-done.halo, f32[4,640]{1,0:T(4,128)} %pad_maximum_fusion.8.vectors, bf16[384,640]{1,0:T(8,128)(2,1)} %bitcast.78, bf16[384,640]{1,0:T(8,128)(2,1)} %copy-done.6, ...), custom_call_target="tpu_custom_call" | custom-call | tf_op jit(solution)/shard_map/conv/pallas_call | solution.py:322
  149.5 12.9 %all-to-all-start = ((bf16[16,32,640]{2,1,0:T(8,128)(2,1)}), bf16[16,32,640]{2,1,0:T(8,128)(2,1)S(1)}, u32[]{:S(2)}, u32[]{:S(2)}) async-start(bf16[16,32,640]{2,1,0:T(8,128)(2,1)} %bitcast.79), calls=%async_computation | async-start | bytes 1310720 | tf_op jit(solution)/shard_map/all_to_all | solution.py:336
  162.5 1.4 pad_maximum_fusion.1
  164.9 1.8 collective-permute-done.29.refs_9_
  166.7 15.7 %all-to-all-done.moved = bf16[16,32,640]{2,1,0:T(8,128)(2,1)S(1)} async-done(((bf16[16,32,640]{2,1,0:T(8,128)(2,1)}), bf16[16,32,640]{2,1,0:T(8,128)(2,1)S(1)}, u32[]{:S(2)}, u32[]{:S(2)}) %all-to-all-start) | async-done | bytes 655392 | tf_op jit(solution)/shard_map/all_to_all | solution.py:336
  182.4 0.8 copy-done.4
  183.2 11.8 %temporal.1 = bf16[16,32,640]{2,1,0:T(8,128)(2,1)} custom-call(s32[4]{0:T(128)} %pad_add_fusion.where, bf16[16,32,640]{2,1,0:T(8,128)(2,1)} %copy-done.4, f32[2,640]{1,0:T(2,128)} %pad_maximum_fusion.9.gains, bf16[288,640]{1,0:T(8,128)(2,1)} %copy-done.2, bf16[288,640]{1,0:T(8,128)(2,1)} %copy-done.10, bf16[288,640]{1,0:T(8,128)(2,1)} %copy-done.12, ...), custom_call_target="tpu_custom_call" | custom-call | tf_op jit(solution)/shard_map/temporal/pallas_call | solution.py:338
  195.0 23.3 %all_to_all.15 = bf16[16,32,640]{2,1,0:T(8,128)(2,1)S(1)} all-to-all(bf16[16,32,640]{2,1,0:T(8,128)(2,1)} %temporal.1), channel_id=1, replica_groups=mesh['groups'=2,'seq_0'=8,'seq_1'=8,'seq_2'=2] {'seq_1','seq_2'}, dimensions={0} | all-to-all | bytes 1310720 | tf_op jit(solution)/shard_map/all_to_all | solution.py:362
  218.3 0.8 copy.33
  (115 shorter events, 7.4 us)
Async XLA Ops:
  0.0 105.2 %copy-start = (bf16[320,640]{1,0:T(8,128)(2,1)S(1)}, bf16[320,640]{1,0:T(8,128)(2,1)}, u32[]{:S(2)}) copy-start(bf16[320,640]{1,0:T(8,128)(2,1)} %param.16) | copy-start | bytes 1228804
  1.6 133.2 %collective-permute-start = (bf16[1,64,640]{2,1,0:T(8,128)(2,1)}, bf16[1,64,640]{2,1,0:T(8,128)(2,1)}, u32[]{:S(2)}, u32[]{:S(2)}) collective-permute-start(bf16[1,64,640]{2,1,0:T(8,128)(2,1)} %constant_dynamic-slice_fusion), channel_id=1, source_target_pairs={{0,64},{1,65},{2,66},{3,67},{4,68},{5,69},{6,70},{7,71},{8,72},{9,... | collective-permute-start | bytes 245768 | tf_op jit(solution)/shard_map/ppermute | solution.py:288
  9.6 18.8 %collective-permute-start.3 = (bf16[10,640]{1,0:T(8,128)(2,1)S(1)}, bf16[10,640]{1,0:T(8,128)(2,1)S(1)}, u32[]{:S(2)}, u32[]{:S(2)}) collective-permute-start(bf16[10,640]{1,0:T(8,128)(2,1)S(1)} %get-tuple-element.14), channel_id=1, source_target_pairs={{0,0},{2,16},{4,32},{6,48},{8,64},{10,80},{12,96},{14,112},{16,2},... | collective-permute-start | bytes 38408 | tf_op jit(solution)/shard_map/ppermute | solution.py:38
  10.3 18.2 %collective-permute-start.4 = (bf16[10,640]{1,0:T(8,128)(2,1)S(1)}, bf16[10,640]{1,0:T(8,128)(2,1)S(1)}, u32[]{:S(2)}, u32[]{:S(2)}) collective-permute-start(bf16[10,640]{1,0:T(8,128)(2,1)S(1)} %get-tuple-element.15), channel_id=1, source_target_pairs={{0,1},{1,0},{2,3},{3,16},{4,5},{5,32},{6,7},{7,48},{8,9},{9,64},{1... | collective-permute-start | bytes 38408 | tf_op jit(solution)/shard_map/ppermute | solution.py:38
  25.1 5.8 %collective-permute-start.2 = (bf16[60,640]{1,0:T(8,128)(2,1)S(1)}, bf16[60,640]{1,0:T(8,128)(2,1)S(1)}, u32[]{:S(2)}, u32[]{:S(2)}) collective-permute-start(bf16[60,640]{1,0:T(8,128)(2,1)S(1)} %pad_maximum_fusion.4), channel_id=1, source_target_pairs={{1,0},{2,1},{3,2},{4,3},{5,4},{6,5},{7,6},{8,7},{9,8},{10,9},{11,1... | collective-permute-start | bytes 230408 | tf_op jit(solution)/shard_map/ppermute | solution.py:38
  29.2 26.8 %copy-start.20 = (s32[4]{0:T(128)S(1)}, s32[4]{0:T(128)}, u32[]{:S(2)}) copy-start(s32[4]{0:T(128)} %param.22) | copy-start | bytes 52
  29.2 29.8 %copy-start.3 = (bf16[8,64,640]{2,1,0:T(8,128)(2,1)S(1)}, bf16[8,64,640]{2,1,0:T(8,128)(2,1)}, u32[]{:S(2)}) copy-start(bf16[8,64,640]{2,1,0:T(8,128)(2,1)} %latents.1) | copy-start | bytes 1966084
  32.6 5.2 %collective-permute-start.5 = (bf16[84,640]{1,0:T(8,128)(2,1)S(1)}, bf16[84,640]{1,0:T(8,128)(2,1)S(1)}, u32[]{:S(2)}, u32[]{:S(2)}) collective-permute-start(bf16[84,640]{1,0:T(8,128)(2,1)S(1)} %pad_maximum_fusion.3), channel_id=1, source_target_pairs={{0,16},{1,3},{2,18},{3,5},{4,20},{5,7},{6,22},{7,9},{8,24},{9,11},... | collective-permute-start | bytes 322568 | tf_op jit(solution)/shard_map/ppermute | solution.py:38
  32.8 5.1 %collective-permute-start.9 = (bf16[84,640]{1,0:T(8,128)(2,1)S(1)}, bf16[84,640]{1,0:T(8,128)(2,1)S(1)}, u32[]{:S(2)}, u32[]{:S(2)}) collective-permute-start(bf16[84,640]{1,0:T(8,128)(2,1)S(1)} %pad_maximum_fusion.3), channel_id=1, source_target_pairs={{0,112},{1,15},{2,114},{3,1},{4,116},{5,3},{6,118},{7,5},{8,120},{... | collective-permute-start | bytes 322568 | tf_op jit(solution)/shard_map/ppermute | solution.py:38
  37.9 5.9 %collective-permute-start.6 = (bf16[84,640]{1,0:T(8,128)(2,1)S(1)}, bf16[84,640]{1,0:T(8,128)(2,1)S(1)}, u32[]{:S(2)}, u32[]{:S(2)}) collective-permute-start(bf16[84,640]{1,0:T(8,128)(2,1)S(1)} %collective-permute-done.5), channel_id=1, source_target_pairs={{0,16},{1,3},{2,18},{3,5},{4,20},{5,7},{6,22},{7,9},{8,24},{9,11},... | collective-permute-start | bytes 322568 | tf_op jit(solution)/shard_map/ppermute | solution.py:38
  37.9 10.7 %collective-permute-start.10 = (bf16[84,640]{1,0:T(8,128)(2,1)S(1)}, bf16[84,640]{1,0:T(8,128)(2,1)S(1)}, u32[]{:S(2)}, u32[]{:S(2)}) collective-permute-start(bf16[84,640]{1,0:T(8,128)(2,1)S(1)} %collective-permute-done.9), channel_id=1, source_target_pairs={{0,112},{1,15},{2,114},{3,1},{4,116},{5,3},{6,118},{7,5},{8,120},{... | collective-permute-start | bytes 322568 | tf_op jit(solution)/shard_map/ppermute | solution.py:38
  43.8 5.6 %collective-permute-start.7 = (bf16[84,640]{1,0:T(8,128)(2,1)S(1)}, bf16[84,640]{1,0:T(8,128)(2,1)S(1)}, u32[]{:S(2)}, u32[]{:S(2)}) collective-permute-start(bf16[84,640]{1,0:T(8,128)(2,1)S(1)} %collective-permute-done.6), channel_id=1, source_target_pairs={{0,16},{1,3},{2,18},{3,5},{4,20},{5,7},{6,22},{7,9},{8,24},{9,11},... | collective-permute-start | bytes 322568 | tf_op jit(solution)/shard_map/ppermute | solution.py:38
  48.6 6.1 %collective-permute-start.11 = (bf16[84,640]{1,0:T(8,128)(2,1)S(1)}, bf16[84,640]{1,0:T(8,128)(2,1)S(1)}, u32[]{:S(2)}, u32[]{:S(2)}) collective-permute-start(bf16[84,640]{1,0:T(8,128)(2,1)S(1)} %collective-permute-done.10), channel_id=1, source_target_pairs={{0,112},{1,15},{2,114},{3,1},{4,116},{5,3},{6,118},{7,5},{8,120},{... | collective-permute-start | bytes 322568 | tf_op jit(solution)/shard_map/ppermute | solution.py:38
  49.3 5.3 %collective-permute-start.8 = (bf16[84,640]{1,0:T(8,128)(2,1)S(1)}, bf16[84,640]{1,0:T(8,128)(2,1)S(1)}, u32[]{:S(2)}, u32[]{:S(2)}) collective-permute-start(bf16[84,640]{1,0:T(8,128)(2,1)S(1)} %collective-permute-done.7), channel_id=1, source_target_pairs={{0,16},{1,3},{2,18},{3,5},{4,20},{5,7},{6,22},{7,9},{8,24},{9,11},... | collective-permute-start | bytes 322568 | tf_op jit(solution)/shard_map/ppermute | solution.py:38
  54.7 15.6 %copy-start.14 = (bf16[8,84,640]{2,1,0:T(8,128)(2,1)}, bf16[8,84,640]{2,1,0:T(8,128)(2,1)S(1)}, u32[]{:S(2)}) copy-start(bf16[8,84,640]{2,1,0:T(8,128)(2,1)S(1)} %bitcast_dynamic-update-slice_fusion.10) | copy-start | bytes 2580484
  54.8 18.9 %copy-start.1 = (bf16[8,48,640]{2,1,0:T(8,128)(2,1)}, bf16[8,48,640]{2,1,0:T(8,128)(2,1)S(1)}, u32[]{:S(2)}) copy-start(bf16[8,48,640]{2,1,0:T(8,128)(2,1)S(1)} %slice.46) | copy-start | bytes 1474564
  54.8 10.2 %collective-permute-start.12 = (bf16[384,640]{1,0:T(8,128)(2,1)S(1)}, bf16[384,640]{1,0:T(8,128)(2,1)S(1)}, u32[]{:S(2)}, u32[]{:S(2)}) collective-permute-start(bf16[384,640]{1,0:T(8,128)(2,1)S(1)} %bitcast.75), channel_id=1, source_target_pairs={{0,2},{1,17},{2,4},{3,19},{4,6},{5,21},{6,8},{7,23},{8,10},{9,25},... | collective-permute-start | bytes 1474568 | tf_op jit(solution)/shard_map/ppermute | solution.py:38
  57.2 13.1 %collective-permute-start.16 = (bf16[384,640]{1,0:T(8,128)(2,1)S(1)}, bf16[384,640]{1,0:T(8,128)(2,1)S(1)}, u32[]{:S(2)}, u32[]{:S(2)}) collective-permute-start(bf16[384,640]{1,0:T(8,128)(2,1)S(1)} %bitcast.76), channel_id=1, source_target_pairs={{0,14},{1,113},{2,0},{3,115},{4,2},{5,117},{6,4},{7,119},{8,6},{9,... | collective-permute-start | bytes 1474568 | tf_op jit(solution)/shard_map/ppermute | solution.py:38
  65.0 9.9 %copy-start.6 = (bf16[384,640]{1,0:T(8,128)(2,1)}, bf16[384,640]{1,0:T(8,128)(2,1)S(1)}, u32[]{:S(2)}) copy-start(bf16[384,640]{1,0:T(8,128)(2,1)S(1)} %collective-permute-done.12.refs_1_) | copy-start | bytes 1474564
  65.0 8.9 %collective-permute-start.13 = (bf16[384,640]{1,0:T(8,128)(2,1)S(1)}, bf16[384,640]{1,0:T(8,128)(2,1)S(1)}, u32[]{:S(2)}, u32[]{:S(2)}) collective-permute-start(bf16[384,640]{1,0:T(8,128)(2,1)S(1)} %collective-permute-done.12.refs_1_), channel_id=1, source_target_pairs={{0,2},{1,17},{2,4},{3,19},{4,6},{5,21},{6,8},{7,23},{8,10},{9,25},... | collective-permute-start | bytes 1474568 | tf_op jit(solution)/shard_map/ppermute | solution.py:38
  70.3 18.7 %copy-start.7 = (bf16[384,640]{1,0:T(8,128)(2,1)}, bf16[384,640]{1,0:T(8,128)(2,1)S(1)}, u32[]{:S(2)}) copy-start(bf16[384,640]{1,0:T(8,128)(2,1)S(1)} %collective-permute-done.16.refs_5_) | copy-start | bytes 1474564
  70.3 18.7 %collective-permute-start.17 = (bf16[384,640]{1,0:T(8,128)(2,1)S(1)}, bf16[384,640]{1,0:T(8,128)(2,1)}, u32[]{:S(2)}, u32[]{:S(2)}) collective-permute-start(bf16[384,640]{1,0:T(8,128)(2,1)S(1)} %collective-permute-done.16.refs_5_), channel_id=1, source_target_pairs={{0,14},{1,113},{2,0},{3,115},{4,2},{5,117},{6,4},{7,119},{8,6},{9,... | collective-permute-start | bytes 1474568 | tf_op jit(solution)/shard_map/ppermute | solution.py:38
  73.9 15.2 %copy-start.8 = (bf16[384,640]{1,0:T(8,128)(2,1)}, bf16[384,640]{1,0:T(8,128)(2,1)S(1)}, u32[]{:S(2)}) copy-start(bf16[384,640]{1,0:T(8,128)(2,1)S(1)} %collective-permute-done.13.refs_2_) | copy-start | bytes 1474564
  73.9 9.2 %collective-permute-start.14 = (bf16[384,640]{1,0:T(8,128)(2,1)S(1)}, bf16[384,640]{1,0:T(8,128)(2,1)}, u32[]{:S(2)}, u32[]{:S(2)}) collective-permute-start(bf16[384,640]{1,0:T(8,128)(2,1)S(1)} %collective-permute-done.13.refs_2_), channel_id=1, source_target_pairs={{0,2},{1,17},{2,4},{3,19},{4,6},{5,21},{6,8},{7,23},{8,10},{9,25},... | collective-permute-start | bytes 1474568 | tf_op jit(solution)/shard_map/ppermute | solution.py:38
  83.0 20.5 %collective-permute-start.15 = (bf16[384,640]{1,0:T(8,128)(2,1)}, bf16[384,640]{1,0:T(8,128)(2,1)S(1)}, u32[]{:S(2)}, u32[]{:S(2)}) collective-permute-start(bf16[384,640]{1,0:T(8,128)(2,1)} %collective-permute-done.14.refs_3_), channel_id=1, source_target_pairs={{0,2},{1,17},{2,4},{3,19},{4,6},{5,21},{6,8},{7,23},{8,10},{9,25},... | collective-permute-start | bytes 1474568 | tf_op jit(solution)/shard_map/ppermute | solution.py:38
  90.9 46.5 %collective-permute-start.19 = (bf16[5,384,640]{2,1,0:T(8,128)(2,1)}, bf16[5,384,640]{2,1,0:T(8,128)(2,1)S(1)}, u32[]{:S(2)}, u32[]{:S(2)}) collective-permute-start(bf16[5,384,640]{2,1,0:T(8,128)(2,1)} %bitcast_dynamic-update-slice_fusion), channel_id=1, source_target_pairs={{0,1},{1,0},{2,3},{3,2},{4,5},{5,4},{6,7},{7,6},{8,9},{9,8},{10,11... | collective-permute-start | bytes 7372808 | tf_op jit(solution)/shard_map/ppermute | solution.py:38
  99.0 8.3 %collective-permute-start.18 = (bf16[384,640]{1,0:T(8,128)(2,1)}, bf16[384,640]{1,0:T(8,128)(2,1)}, u32[]{:S(2)}, u32[]{:S(2)}) collective-permute-start(bf16[384,640]{1,0:T(8,128)(2,1)} %collective-permute-done.17.refs_6_), channel_id=1, source_target_pairs={{0,14},{1,113},{2,0},{3,115},{4,2},{5,117},{6,4},{7,119},{8,6},{9,... | collective-permute-start | bytes 1474568 | tf_op jit(solution)/shard_map/ppermute | solution.py:38
  103.5 9.7 %copy-start.2 = (bf16[288,640]{1,0:T(8,128)(2,1)}, bf16[288,640]{1,0:T(8,128)(2,1)S(1)}, u32[]{:S(2)}) copy-start(bf16[288,640]{1,0:T(8,128)(2,1)S(1)} %pad_maximum_fusion.2.refs_0_) | copy-start | bytes 1105924
  103.6 9.7 %copy-start.9 = (bf16[384,640]{1,0:T(8,128)(2,1)}, bf16[384,640]{1,0:T(8,128)(2,1)S(1)}, u32[]{:S(2)}) copy-start(bf16[384,640]{1,0:T(8,128)(2,1)S(1)} %collective-permute-done.15.refs_4_) | copy-start | bytes 1474564
  103.6 8.9 %collective-permute-start.21 = (bf16[288,640]{1,0:T(8,128)(2,1)S(1)}, bf16[288,640]{1,0:T(8,128)(2,1)S(1)}, u32[]{:S(2)}, u32[]{:S(2)}) collective-permute-start(bf16[288,640]{1,0:T(8,128)(2,1)S(1)} %pad_maximum_fusion.2.refs_0_), channel_id=1, source_target_pairs={{0,2},{1,17},{2,4},{3,19},{4,6},{5,21},{6,8},{7,23},{8,10},{9,25},... | collective-permute-start | bytes 1105928 | tf_op jit(solution)/shard_map/ppermute | solution.py:38
  105.5 7.8 %collective-permute-start.25 = (bf16[288,640]{1,0:T(8,128)(2,1)S(1)}, bf16[288,640]{1,0:T(8,128)(2,1)S(1)}, u32[]{:S(2)}, u32[]{:S(2)}) collective-permute-start(bf16[288,640]{1,0:T(8,128)(2,1)S(1)} %pad_maximum_fusion.2.refs_0_), channel_id=1, source_target_pairs={{0,14},{1,113},{2,0},{3,115},{4,2},{5,117},{6,4},{7,119},{8,6},{9,... | collective-permute-start | bytes 1105928 | tf_op jit(solution)/shard_map/ppermute | solution.py:38
  109.9 24.8 %copy-start.17 = (f32[640]{0:T(1024)S(1)}, f32[640]{0:T(1024)}, u32[]{:S(2)}) copy-start(f32[640]{0:T(1024)} %param.14) | copy-start | bytes 7684
  109.9 26.6 %copy-start.16 = (f32[640]{0:T(1024)S(1)}, f32[640]{0:T(1024)}, u32[]{:S(2)}) copy-start(f32[640]{0:T(1024)} %param.13) | copy-start | bytes 7684
  109.9 27.5 %collective-permute-start.20 = (bf16[3,384,640]{2,1,0:T(8,128)(2,1)}, bf16[3,384,640]{2,1,0:T(8,128)(2,1)}, u32[]{:S(2)}, u32[]{:S(2)}) collective-permute-start(bf16[3,384,640]{2,1,0:T(8,128)(2,1)} %pad_maximum_fusion), channel_id=1, source_target_pairs={{0,1},{1,0},{2,3},{3,2},{4,5},{5,4},{6,7},{7,6},{8,9},{9,8},{10,11... | collective-permute-start | bytes 4423688 | tf_op jit(solution)/shard_map/ppermute | solution.py:38
  112.4 21.7 %copy-start.10 = (bf16[288,640]{1,0:T(8,128)(2,1)}, bf16[288,640]{1,0:T(8,128)(2,1)S(1)}, u32[]{:S(2)}) copy-start(bf16[288,640]{1,0:T(8,128)(2,1)S(1)} %collective-permute-done.21.refs_1_) | copy-start | bytes 1105924
  112.4 7.9 %collective-permute-start.22 = (bf16[288,640]{1,0:T(8,128)(2,1)S(1)}, bf16[288,640]{1,0:T(8,128)(2,1)S(1)}, u32[]{:S(2)}, u32[]{:S(2)}) collective-permute-start(bf16[288,640]{1,0:T(8,128)(2,1)S(1)} %collective-permute-done.21.refs_1_), channel_id=1, source_target_pairs={{0,2},{1,17},{2,4},{3,19},{4,6},{5,21},{6,8},{7,23},{8,10},{9,25},... | collective-permute-start | bytes 1105928 | tf_op jit(solution)/shard_map/ppermute | solution.py:38
  113.3 20.8 %copy-start.11 = (bf16[288,640]{1,0:T(8,128)(2,1)}, bf16[288,640]{1,0:T(8,128)(2,1)S(1)}, u32[]{:S(2)}) copy-start(bf16[288,640]{1,0:T(8,128)(2,1)S(1)} %collective-permute-done.25.refs_5_) | copy-start | bytes 1105924
  113.3 8.7 %collective-permute-start.26 = (bf16[288,640]{1,0:T(8,128)(2,1)S(1)}, bf16[288,640]{1,0:T(8,128)(2,1)S(1)}, u32[]{:S(2)}, u32[]{:S(2)}) collective-permute-start(bf16[288,640]{1,0:T(8,128)(2,1)S(1)} %collective-permute-done.25.refs_5_), channel_id=1, source_target_pairs={{0,14},{1,113},{2,0},{3,115},{4,2},{5,117},{6,4},{7,119},{8,6},{9,... | collective-permute-start | bytes 1105928 | tf_op jit(solution)/shard_map/ppermute | solution.py:38
  120.3 13.8 %copy-start.12 = (bf16[288,640]{1,0:T(8,128)(2,1)}, bf16[288,640]{1,0:T(8,128)(2,1)S(1)}, u32[]{:S(2)}) copy-start(bf16[288,640]{1,0:T(8,128)(2,1)S(1)} %collective-permute-done.22.refs_2_) | copy-start | bytes 1105924
  120.3 14.6 %collective-permute-start.23 = (bf16[288,640]{1,0:T(8,128)(2,1)S(1)}, bf16[288,640]{1,0:T(8,128)(2,1)}, u32[]{:S(2)}, u32[]{:S(2)}) collective-permute-start(bf16[288,640]{1,0:T(8,128)(2,1)S(1)} %collective-permute-done.22.refs_2_), channel_id=1, source_target_pairs={{0,2},{1,17},{2,4},{3,19},{4,6},{5,21},{6,8},{7,23},{8,10},{9,25},... | collective-permute-start | bytes 1105928 | tf_op jit(solution)/shard_map/ppermute | solution.py:38
  122.0 27.5 %copy-start.13 = (bf16[288,640]{1,0:T(8,128)(2,1)}, bf16[288,640]{1,0:T(8,128)(2,1)S(1)}, u32[]{:S(2)}) copy-start(bf16[288,640]{1,0:T(8,128)(2,1)S(1)} %collective-permute-done.26.refs_6_) | copy-start | bytes 1105924
  122.0 9.8 %collective-permute-start.1 = (f32[2,32]{1,0:T(2,128)S(1)}, f32[2,32]{1,0:T(2,128)S(1)}, u32[]{:S(2)}, u32[]{:S(2)}) collective-permute-start(f32[2,32]{1,0:T(2,128)S(1)} %maximum_reduce_fusion), channel_id=1, source_target_pairs={{0,64},{1,65},{2,66},{3,67},{4,68},{5,69},{6,70},{7,71},{8,72},{9,... | collective-permute-start | bytes 776 | tf_op jit(solution)/shard_map/ppermute | solution.py:292
  131.8 33.1 %collective-permute-start.28 = (bf16[5,288,640]{2,1,0:T(8,128)(2,1)}, bf16[5,288,640]{2,1,0:T(8,128)(2,1)}, u32[]{:S(2)}, u32[]{:S(2)}) collective-permute-start(bf16[5,288,640]{2,1,0:T(8,128)(2,1)} %bitcast_dynamic-update-slice_fusion.5), channel_id=1, source_target_pairs={{0,1},{1,0},{2,3},{3,2},{4,5},{5,4},{6,7},{7,6},{8,9},{9,8},{10,11... | collective-permute-start | bytes 5529608 | tf_op jit(solution)/shard_map/ppermute | solution.py:38
  134.7 27.7 %collective-permute-start.27 = (bf16[288,640]{1,0:T(8,128)(2,1)S(1)}, bf16[288,640]{1,0:T(8,128)(2,1)}, u32[]{:S(2)}, u32[]{:S(2)}) collective-permute-start(bf16[288,640]{1,0:T(8,128)(2,1)S(1)} %collective-permute-done.26.refs_6_), channel_id=1, source_target_pairs={{0,14},{1,113},{2,0},{3,115},{4,2},{5,117},{6,4},{7,119},{8,6},{9,... | collective-permute-start | bytes 1105928 | tf_op jit(solution)/shard_map/ppermute | solution.py:38
  134.9 27.6 %collective-permute-start.24 = (bf16[288,640]{1,0:T(8,128)(2,1)}, bf16[288,640]{1,0:T(8,128)(2,1)}, u32[]{:S(2)}, u32[]{:S(2)}) collective-permute-start(bf16[288,640]{1,0:T(8,128)(2,1)} %collective-permute-done.23.refs_3_), channel_id=1, source_target_pairs={{0,2},{1,17},{2,4},{3,19},{4,6},{5,21},{6,8},{7,23},{8,10},{9,25},... | collective-permute-start | bytes 1105928 | tf_op jit(solution)/shard_map/ppermute | solution.py:38
  137.4 1.4 copy-start.5
  149.5 14.8 %copy-start.18 = (f32[640]{0:T(1024)S(1)}, f32[640]{0:T(1024)}, u32[]{:S(2)}) copy-start(f32[640]{0:T(1024)} %param.19) | copy-start | bytes 7684
  149.5 14.7 %copy-start.19 = (f32[640]{0:T(1024)S(1)}, f32[640]{0:T(1024)}, u32[]{:S(2)}) copy-start(f32[640]{0:T(1024)} %param.17) | copy-start | bytes 7684
  149.5 32.9 %all-to-all-start = ((bf16[16,32,640]{2,1,0:T(8,128)(2,1)}), bf16[16,32,640]{2,1,0:T(8,128)(2,1)S(1)}, u32[]{:S(2)}, u32[]{:S(2)}) async-start(bf16[16,32,640]{2,1,0:T(8,128)(2,1)} %bitcast.79), calls=%async_computation | async-start | bytes 1310720 | tf_op jit(solution)/shard_map/all_to_all | solution.py:336
  163.8 2.9 %collective-permute-start.29 = (bf16[3,288,640]{2,1,0:T(8,128)(2,1)S(1)}, bf16[3,288,640]{2,1,0:T(8,128)(2,1)S(1)}, u32[]{:S(2)}, u32[]{:S(2)}) collective-permute-start(bf16[3,288,640]{2,1,0:T(8,128)(2,1)S(1)} %pad_maximum_fusion.1), channel_id=1, source_target_pairs={{0,1},{1,0},{2,3},{3,2},{4,5},{5,4},{6,7},{7,6},{8,9},{9,8},{10,11... | collective-permute-start | bytes 3317768 | tf_op jit(solution)/shard_map/ppermute | solution.py:38
  166.7 15.7 %copy-start.15 = (bf16[3,288,640]{2,1,0:T(8,128)(2,1)}, bf16[3,288,640]{2,1,0:T(8,128)(2,1)S(1)}, u32[]{:S(2)}) copy-start(bf16[3,288,640]{2,1,0:T(8,128)(2,1)S(1)} %collective-permute-done.29.refs_9_) | copy-start | bytes 3317764
  182.4 0.8 copy-start.4
